TPU v7x, 32 devices: a whole 2x2x4 slice. The times are simulated.
32 devices in a mesh: gx: 8 (over y, x, core), gy: 4 (over z).
Axes of the slice: x: 2, y: 2, z: 4, core: 2. Of those that a mesh axis runs over, the one named last changes fastest.
Arguments:
- probes: float32 [16, 128, 128, 256], P(None, 'gx', 'gy'), may hold values from -6 to 6
- diffusivity: float32 [128, 128, 256], P('gx', 'gy'), may hold values from 0.5 to 2
- wind_speed: float32 [3], replicated, may hold values from 0.5 to 2
- sensor_cell: int32 [8, 4, 128], P('gx', 'gy'), may hold values from 0 to 131071
- sensor_owner: int32 [8, 4, 128, 1], P('gx', 'gy'), may hold values from 0 to 31; in each aligned block of 128 rows (0 to 127, 128 to 255, ..., all dimensions but the last counted through in order) at most 4 rows name the same one
- sensor_count: int32 [8, 4], P('gx', 'gy'), may hold values from 64 to 128
- goal_weight: float32 [8, 4, 128, 16], P('gx', 'gy'), may hold values from -0.6 to 0.6
Outputs:
- fields: float32 [16, 128, 128, 256], P(None, 'gx', 'gy')
- goal_block: float32 [512, 16], P(('gx', 'gy'))
- ritz_gram: float32 [16, 16], replicated
Inputs may be any that keep to these rules, and one draw needn't show every extreme that they name: `sensor_owner`: among the rows of one device, no owner is named more than 4 times, a bound that some block reaches.
All inputs are finite; a program needn't handle non-finite values.
Results may differ from a plain program's by a relative error of at most 0.0003.
Values sent between devices are 32-bit elements; how exact they have to be, the bound alone decides.
A program may use at most 192 MiB of HBM per device.

v0:
```python
import jax
import jax.numpy as jnp
from jax import lax
from jax.sharding import PartitionSpec as P

STEPS = 2
SWEEPS = 4


time_step = 2.0


def padded_2(cells, sides, width):
    for axis, dim in sides:
        count = lax.axis_size(axis)
        ends = count - 1
        head = lax.slice_in_dim(cells, 0, width, axis=dim)
        tail = lax.slice_in_dim(cells, cells.shape[dim] - width, cells.shape[dim], axis=dim)
        cells = jnp.concatenate(
            [
                lax.ppermute(tail, axis, [(i, (i + 1) % count) for i in range(ends)]),
                cells,
                lax.ppermute(head, axis, [((i + 1) % count, i) for i in range(ends)]),
            ],
            axis=dim,
        )
    return cells


def relax(padded, source, diffusion, wind_speed):
    centre = padded[..., 1:-1, 1:-1, :]
    widths = [(0, 0)] * (centre.ndim - 1) + [(1, 1)]
    zpadded = jnp.pad(centre, widths)
    beside = padded[..., 2:, 1:-1, :] + padded[..., :-2, 1:-1, :]
    beside = beside + padded[..., 1:-1, 2:, :] + padded[..., 1:-1, :-2, :]
    beside = beside + zpadded[..., 2:] + zpadded[..., :-2]
    upwind = (
        wind_speed[0] * padded[..., :-2, 1:-1, :]
        + wind_speed[1] * padded[..., 1:-1, :-2, :]
        + wind_speed[2] * zpadded[..., :-2]
    )
    diagonal = 1.0 + time_step * (6.0 * diffusion + wind_speed[0] + wind_speed[1] + wind_speed[2])
    updated = (source + time_step * (diffusion * beside + upwind)) / diagonal
    return jnp.where(diffusion > 0.0, updated, 0.0)


def body(probes, diffusivity, wind_speed, sensor_cell, sensor_owner, sensor_count, goal_weight):
    state_field = probes
    for step_index in range(STEPS):
        source = state_field
        for sweep_index in range(SWEEPS):
            padded = padded_2(state_field, (("gx", 1), ("gy", 2)), 1)
            state_field = relax(padded, source, diffusivity, wind_speed)
    probe_count = state_field.shape[0]
    sensor_rows = sensor_cell.shape[2]
    goal_count = goal_weight.shape[3]
    device_count = lax.axis_size("gx") * lax.axis_size("gy")
    capacity = max(2, (sensor_rows + device_count - 1) // device_count)
    flattened = state_field.reshape(probe_count, -1)
    readings = jnp.take(flattened, sensor_cell.reshape(-1), axis=1)
    row_index = jnp.arange(sensor_rows, dtype=jnp.int32)
    active = (row_index < sensor_count.reshape(())).astype(jnp.float32)
    readings = readings.T * active[:, None]
    weights = goal_weight.reshape(sensor_rows, goal_count)
    owners = sensor_owner.reshape(sensor_rows)
    earlier = (owners[None, :] == owners[:, None]) & (row_index[None, :] < row_index[:, None])
    slot_rank = jnp.sum(earlier.astype(jnp.int32), axis=1)
    slot_index = owners * capacity + slot_rank
    placing = (
        jnp.arange(device_count * capacity, dtype=jnp.int32)[:, None] == slot_index[None, :]
    ).astype(jnp.float32)
    payload = jnp.concatenate([readings, weights], axis=1)
    outgoing = jnp.dot(placing, payload, precision=lax.Precision.HIGHEST).reshape(
        device_count, capacity, probe_count + goal_count
    )
    received = lax.all_to_all(outgoing, ("gx", "gy"), split_axis=0, concat_axis=0, tiled=True)
    goal_block = jnp.einsum(
        "scj,scp->jp",
        received[..., probe_count:],
        received[..., :probe_count],
        precision=lax.Precision.HIGHEST,
    )
    ritz_gram = lax.psum(
        jnp.dot(goal_block.T, goal_block, precision=lax.Precision.HIGHEST), ("gx", "gy")
    )
    return (state_field, goal_block, ritz_gram)


def solution(mesh):
    placed = (
        P(None, "gx", "gy", None),
        P("gx", "gy", None),
        P(),
        P("gx", "gy", None),
        P("gx", "gy", None, None),
        P("gx", "gy"),
        P("gx", "gy", None, None),
    )
    return jax.shard_map(
        body,
        mesh=mesh,
        in_specs=placed,
        out_specs=(P(None, "gx", "gy", None), P(("gx", "gy"), None), P()),
        check_vma=False,
    )
```

profile of v0, /device:TPU:0, one launch (start us, length us, event | category | flops | bytes accessed | tf_op | source)
XLA Modules:
  0.0 529.9 jit_solution(1779432885856855623)
XLA Ops:
  0.7 10.1 %copy.60 = f32[16,16,32,256]{3,0,2,1:T(8,128)S(1)} copy(f32[16,16,32,256]{3,2,1,0:T(8,128)} %param.7) | data formatting | bytes 16777216 | tf_op args[0]
  15.7 10.0 %constant_dynamic-update-slice_fusion.1 = f32[16,18,32,256]{3,0,2,1:T(8,128)} fusion(f32[16,18,32,256]{3,0,2,1:T(8,128)} %constant_dynamic-update-slice_fusion.2, f32[16,16,32,256]{3,2,1,0:T(8,128)S(1)} %copy-done), kind=kLoop, calls=%fused_computation.202 | loop fusion | bytes 16777216
  28.9 4.9 collective-permute-start.3
  38.1 25.3 %fusion.81 = f32[16,16,32,256]{3,0,2,1:T(8,128)} fusion(f32[16,16,32,256]{3,0,2,1:T(8,128)} %copy-done.2, f32[16,18,32,256]{3,0,2,1:T(8,128)} %constant_dynamic-update-slice_fusion, f32[16,18,1,256]{3,0,2,1:T(8,128)S(1)} %collective-permute-done.3, f32[16,18,1,256]{3,0,2,1:T(8,128)S(1)} %collective-permute-done.2, ...), kind=kLoop, calls=%fused_computation.158 | loop fusion | flops 41943040 | bytes 29032460 | tf_op jit(solution)/shard_map/jit(_where)/select_n | solution.py:44
  66.0 8.1 %collective-permute-start.5 = (f32[16,1,32,256]{3,0,2,1:T(8,128)S(1)}, f32[16,1,32,256]{3,0,2,1:T(8,128)S(1)}, u32[]{:S(2)}, u32[]{:S(2)}) collective-permute-start(f32[16,1,32,256]{3,0,2,1:T(8,128)S(1)} %get-tuple-element.40), channel_id=1, source_target_pairs={{0,4},{4,8},{8,12},{12,16},{16,20},{20,24},{24,28},{1,5},{5,9},{9,... | collective-permute-start | bytes 1572872 | tf_op jit(solution)/shard_map/ppermute | solution.py:21
  78.0 4.9 collective-permute-start.7
  86.9 24.8 %fusion.87 = f32[16,16,32,256]{3,0,2,1:T(8,128)} fusion(f32[16,16,32,256]{3,0,2,1:T(8,128)} %fusion.81, f32[16,1,32,256]{3,0,2,1:T(8,128)S(1)} %collective-permute-done.4, f32[16,1,32,256]{3,0,2,1:T(8,128)S(1)} %collective-permute-done.5, f32[16,18,1,256]{3,0,2,1:T(8,128)S(1)} %collective-permute-done.7, f32[16,18,1,256]{3,0,2,1:T(8,128)S(1)} %collective-permute-done.6, ...), kind=kLoop, calls=%fused_computation.164 | loop fusion | flops 50331648 | bytes 27983884 | tf_op jit(solution)/shard_map/jit(_where)/select_n | solution.py:44
  114.4 12.9 %collective-permute-start.9 = (f32[16,1,32,256]{3,0,2,1:T(8,128)S(1)}, f32[16,1,32,256]{3,0,2,1:T(8,128)S(1)}, u32[]{:S(2)}, u32[]{:S(2)}) collective-permute-start(f32[16,1,32,256]{3,0,2,1:T(8,128)S(1)} %get-tuple-element.38), channel_id=1, source_target_pairs={{0,4},{4,8},{8,12},{12,16},{16,20},{20,24},{24,28},{1,5},{5,9},{9,... | collective-permute-start | bytes 1572872 | tf_op jit(solution)/shard_map/ppermute | solution.py:21
  140.1 24.8 %fusion.86 = f32[16,16,32,256]{3,0,2,1:T(8,128)} fusion(f32[16,16,32,256]{3,0,2,1:T(8,128)} %fusion.87, f32[16,1,32,256]{3,0,2,1:T(8,128)S(1)} %collective-permute-done.8, f32[16,1,32,256]{3,0,2,1:T(8,128)S(1)} %collective-permute-done.9, f32[16,18,1,256]{3,0,2,1:T(8,128)S(1)} %collective-permute-done.11, ...), kind=kLoop, calls=%fused_computation.163 | loop fusion | flops 50331648 | bytes 27983884 | tf_op jit(solution)/shard_map/jit(_where)/select_n | solution.py:44
  167.4 10.1 %collective-permute-start.13 = (f32[16,1,32,256]{3,0,2,1:T(8,128)S(1)}, f32[16,1,32,256]{3,0,2,1:T(8,128)S(1)}, u32[]{:S(2)}, u32[]{:S(2)}) collective-permute-start(f32[16,1,32,256]{3,0,2,1:T(8,128)S(1)} %get-tuple-element.36), channel_id=1, source_target_pairs={{0,4},{4,8},{8,12},{12,16},{16,20},{20,24},{24,28},{1,5},{5,9},{9,... | collective-permute-start | bytes 1572872 | tf_op jit(solution)/shard_map/ppermute | solution.py:21
  190.5 24.2 %fusion.85 = f32[16,16,32,256]{3,0,2,1:T(8,128)S(1)} fusion(f32[16,16,32,256]{3,0,2,1:T(8,128)} %fusion.86, f32[16,1,32,256]{3,0,2,1:T(8,128)S(1)} %collective-permute-done.12, f32[16,1,32,256]{3,0,2,1:T(8,128)S(1)} %collective-permute-done.13, f32[16,18,1,256]{3,0,2,1:T(8,128)S(1)} %collective-permute-done.15, ...), kind=kLoop, calls=%fused_computation.162 | loop fusion | flops 50331648 | bytes 27983884 | tf_op jit(solution)/shard_map/jit(_where)/select_n | solution.py:44
  216.1 9.8 %collective-permute-start.17 = (f32[16,1,32,256]{3,0,2,1:T(8,128)S(1)}, f32[16,1,32,256]{3,0,2,1:T(8,128)S(1)}, u32[]{:S(2)}, u32[]{:S(2)}) collective-permute-start(f32[16,1,32,256]{3,0,2,1:T(8,128)S(1)} %get-tuple-element.34), channel_id=1, source_target_pairs={{0,4},{4,8},{8,12},{12,16},{16,20},{20,24},{24,28},{1,5},{5,9},{9,... | collective-permute-start | bytes 1572872 | tf_op jit(solution)/shard_map/ppermute | solution.py:21
  228.7 5.2 collective-permute-start.19
  237.8 13.1 %fusion.80 = f32[16,16,32,256]{3,0,2,1:T(8,128)} fusion(f32[16,16,32,256]{3,0,2,1:T(8,128)S(1)} %fusion.85, f32[16,1,32,256]{3,0,2,1:T(8,128)S(1)} %collective-permute-done.16, f32[16,1,32,256]{3,0,2,1:T(8,128)S(1)} %collective-permute-done.17, f32[16,18,1,256]{3,0,2,1:T(8,128)S(1)} %collective-permute-done.19, ...), kind=kLoop, calls=%fused_computation.157 | loop fusion | flops 50331648 | bytes 19595276 | tf_op jit(solution)/shard_map/jit(_where)/select_n | solution.py:44
  253.5 9.8 %collective-permute-start.21 = (f32[16,1,32,256]{3,0,2,1:T(8,128)S(1)}, f32[16,1,32,256]{3,0,2,1:T(8,128)S(1)}, u32[]{:S(2)}, u32[]{:S(2)}) collective-permute-start(f32[16,1,32,256]{3,0,2,1:T(8,128)S(1)} %get-tuple-element.32), channel_id=1, source_target_pairs={{0,4},{4,8},{8,12},{12,16},{16,20},{20,24},{24,28},{1,5},{5,9},{9,... | collective-permute-start | bytes 1572872 | tf_op jit(solution)/shard_map/ppermute | solution.py:21
  276.2 22.7 %fusion.84 = f32[16,16,32,256]{3,0,2,1:T(8,128)} fusion(f32[16,16,32,256]{3,0,2,1:T(8,128)S(1)} %fusion.85, f32[16,16,32,256]{3,0,2,1:T(8,128)} %fusion.80, f32[16,1,32,256]{3,0,2,1:T(8,128)S(1)} %collective-permute-done.20, f32[16,1,32,256]{3,0,2,1:T(8,128)S(1)} %collective-permute-done.21, f32[16,18,1,256]{3,0,2,1:T(8,128)S(1)} %collective-permute-done.23, ...), kind=kLoop, calls=%fused_computation.161 | loop fusion | flops 50331648 | bytes 27983884 | tf_op jit(solution)/shard_map/jit(_where)/select_n | solution.py:44
  301.5 11.3 %collective-permute-start.25 = (f32[16,1,32,256]{3,0,2,1:T(8,128)S(1)}, f32[16,1,32,256]{3,0,2,1:T(8,128)S(1)}, u32[]{:S(2)}, u32[]{:S(2)}) collective-permute-start(f32[16,1,32,256]{3,0,2,1:T(8,128)S(1)} %get-tuple-element.30), channel_id=1, source_target_pairs={{0,4},{4,8},{8,12},{12,16},{16,20},{20,24},{24,28},{1,5},{5,9},{9,... | collective-permute-start | bytes 1572872 | tf_op jit(solution)/shard_map/ppermute | solution.py:21
  325.6 22.7 %fusion.83 = f32[16,16,32,256]{3,0,2,1:T(8,128)} fusion(f32[16,16,32,256]{3,0,2,1:T(8,128)S(1)} %fusion.85, f32[16,16,32,256]{3,0,2,1:T(8,128)} %fusion.84, f32[16,1,32,256]{3,0,2,1:T(8,128)S(1)} %collective-permute-done.24, f32[16,1,32,256]{3,0,2,1:T(8,128)S(1)} %collective-permute-done.25, f32[16,18,1,256]{3,0,2,1:T(8,128)S(1)} %collective-permute-done.27, ...), kind=kLoop, calls=%fused_computation.160 | loop fusion | flops 50331648 | bytes 27983884 | tf_op jit(solution)/shard_map/jit(_where)/select_n | solution.py:44
  350.9 13.9 %collective-permute-start.29 = (f32[16,1,32,256]{3,0,2,1:T(8,128)S(1)}, f32[16,1,32,256]{3,0,2,1:T(8,128)S(1)}, u32[]{:S(2)}, u32[]{:S(2)}) collective-permute-start(f32[16,1,32,256]{3,0,2,1:T(8,128)S(1)} %get-tuple-element.28), channel_id=1, source_target_pairs={{0,4},{4,8},{8,12},{12,16},{16,20},{20,24},{24,28},{1,5},{5,9},{9,... | collective-permute-start | bytes 1572872 | tf_op jit(solution)/shard_map/ppermute | solution.py:21
  377.7 22.7 %fusion.82 = f32[16,16,32,256]{3,0,2,1:T(8,128)} fusion(f32[16,16,32,256]{3,0,2,1:T(8,128)S(1)} %fusion.85, f32[16,16,32,256]{3,0,2,1:T(8,128)} %fusion.83, f32[16,1,32,256]{3,0,2,1:T(8,128)S(1)} %collective-permute-done.28, f32[16,1,32,256]{3,0,2,1:T(8,128)S(1)} %collective-permute-done.29, f32[16,18,1,256]{3,0,2,1:T(8,128)S(1)} %collective-permute-done.31, ...), kind=kLoop, calls=%fused_computation.159 | loop fusion | flops 50331648 | bytes 27983884 | tf_op jit(solution)/shard_map/jit(_where)/select_n | solution.py:44
  400.4 32.9 %copy.61 = f32[16,16,32,256]{0,3,2,1:T(8,128)} copy(f32[16,16,32,256]{3,0,2,1:T(8,128)} %fusion.82) | data formatting | bytes 16777216 | tf_op jit(solution)/shard_map/jit(_where)/select_n | solution.py:44
  436.0 39.6 %all-to-all-start = ((f32[32,1,128]{2,1,0:T(1,128)}), f32[32,1,128]{2,1,0:T(1,128)S(1)}, u32[]{:S(2)}, u32[]{:S(2)}) async-start(f32[32,1,128]{2,1,0:T(1,128)} %reshape.93), calls=%async_computation | async-start | bytes 32768 | tf_op jit(solution)/shard_map/all_to_all | solution.py:76
  475.6 11.6 %copy.66 = f32[16,16,32,256]{3,2,1,0:T(8,128)} copy(f32[16,16,32,256]{3,0,2,1:T(8,128)} %fusion.82) | data formatting | bytes 16777216
  489.1 40.6 %psum.7 = f32[16,16]{1,0:T(8,128)} all-reduce(f32[16,16]{1,0:T(8,128)S(1)} %fusion.109), channel_id=1, replica_groups=mesh['gx'=8,'gy'=4] {'gx','gy'}, use_global_device_ids=true, to_apply=%region_1.2 | all-reduce | flops 256 | bytes 2048 | tf_op jit(solution)/shard_map/psum | solution.py:83
  (108 shorter events, 111.4 us)
Async XLA Ops:
  13.3 12.4 %collective-permute-start = (f32[16,1,32,256]{3,0,2,1:T(8,128)S(1)}, f32[16,1,32,256]{3,0,2,1:T(8,128)S(1)}, u32[]{:S(2)}, u32[]{:S(2)}) collective-permute-start(f32[16,1,32,256]{3,0,2,1:T(8,128)S(1)} %get-tuple-element.42), channel_id=1, source_target_pairs={{4,0},{8,4},{12,8},{16,12},{20,16},{24,20},{28,24},{5,1},{9,5},{13... | collective-permute-start | bytes 1572872 | tf_op jit(solution)/shard_map/ppermute | solution.py:23
  27.6 9.0 %collective-permute-start.2 = (f32[16,18,1,256]{3,0,2,1:T(8,128)S(1)}, f32[16,18,1,256]{3,0,2,1:T(8,128)S(1)}, u32[]{:S(2)}, u32[]{:S(2)}) collective-permute-start(f32[16,18,1,256]{3,0,2,1:T(8,128)S(1)} %get-tuple-element.26), channel_id=1, source_target_pairs={{1,0},{2,1},{3,2},{5,4},{6,5},{7,6},{9,8},{10,9},{11,10},{13,12},{... | collective-permute-start | bytes 884744 | tf_op jit(solution)/shard_map/ppermute | solution.py:23
  28.9 9.2 %collective-permute-start.3 = (f32[16,18,1,256]{3,0,2,1:T(8,128)S(1)}, f32[16,18,1,256]{3,0,2,1:T(8,128)S(1)}, u32[]{:S(2)}, u32[]{:S(2)}) collective-permute-start(f32[16,18,1,256]{3,0,2,1:T(8,128)S(1)} %get-tuple-element.27), channel_id=1, source_target_pairs={{0,1},{1,2},{2,3},{4,5},{5,6},{6,7},{8,9},{9,10},{10,11},{12,13},{... | collective-permute-start | bytes 884744 | tf_op jit(solution)/shard_map/ppermute | solution.py:21
  64.7 9.5 %collective-permute-start.4 = (f32[16,1,32,256]{3,0,2,1:T(8,128)S(1)}, f32[16,1,32,256]{3,0,2,1:T(8,128)S(1)}, u32[]{:S(2)}, u32[]{:S(2)}) collective-permute-start(f32[16,1,32,256]{3,0,2,1:T(8,128)S(1)} %get-tuple-element.41), channel_id=1, source_target_pairs={{4,0},{8,4},{12,8},{16,12},{20,16},{24,20},{28,24},{5,1},{9,5},{13... | collective-permute-start | bytes 1572872 | tf_op jit(solution)/shard_map/ppermute | solution.py:23
  66.0 9.6 %collective-permute-start.5 = (f32[16,1,32,256]{3,0,2,1:T(8,128)S(1)}, f32[16,1,32,256]{3,0,2,1:T(8,128)S(1)}, u32[]{:S(2)}, u32[]{:S(2)}) collective-permute-start(f32[16,1,32,256]{3,0,2,1:T(8,128)S(1)} %get-tuple-element.40), channel_id=1, source_target_pairs={{0,4},{4,8},{8,12},{12,16},{16,20},{20,24},{24,28},{1,5},{5,9},{9,... | collective-permute-start | bytes 1572872 | tf_op jit(solution)/shard_map/ppermute | solution.py:21
  78.0 8.9 %collective-permute-start.7 = (f32[16,18,1,256]{3,0,2,1:T(8,128)S(1)}, f32[16,18,1,256]{3,0,2,1:T(8,128)S(1)}, u32[]{:S(2)}, u32[]{:S(2)}) collective-permute-start(f32[16,18,1,256]{3,0,2,1:T(8,128)S(1)} %get-tuple-element.25), channel_id=1, source_target_pairs={{0,1},{1,2},{2,3},{4,5},{5,6},{6,7},{8,9},{9,10},{10,11},{12,13},{... | collective-permute-start | bytes 884744 | tf_op jit(solution)/shard_map/ppermute | solution.py:21
  113.1 14.2 %collective-permute-start.8 = (f32[16,1,32,256]{3,0,2,1:T(8,128)S(1)}, f32[16,1,32,256]{3,0,2,1:T(8,128)S(1)}, u32[]{:S(2)}, u32[]{:S(2)}) collective-permute-start(f32[16,1,32,256]{3,0,2,1:T(8,128)S(1)} %get-tuple-element.39), channel_id=1, source_target_pairs={{4,0},{8,4},{12,8},{16,12},{20,16},{24,20},{28,24},{5,1},{9,5},{13... | collective-permute-start | bytes 1572872 | tf_op jit(solution)/shard_map/ppermute | solution.py:23
  114.4 14.4 %collective-permute-start.9 = (f32[16,1,32,256]{3,0,2,1:T(8,128)S(1)}, f32[16,1,32,256]{3,0,2,1:T(8,128)S(1)}, u32[]{:S(2)}, u32[]{:S(2)}) collective-permute-start(f32[16,1,32,256]{3,0,2,1:T(8,128)S(1)} %get-tuple-element.38), channel_id=1, source_target_pairs={{0,4},{4,8},{8,12},{12,16},{16,20},{20,24},{24,28},{1,5},{5,9},{9,... | collective-permute-start | bytes 1572872 | tf_op jit(solution)/shard_map/ppermute | solution.py:21
  131.2 8.9 %collective-permute-start.11 = (f32[16,18,1,256]{3,0,2,1:T(8,128)S(1)}, f32[16,18,1,256]{3,0,2,1:T(8,128)S(1)}, u32[]{:S(2)}, u32[]{:S(2)}) collective-permute-start(f32[16,18,1,256]{3,0,2,1:T(8,128)S(1)} %get-tuple-element.23), channel_id=1, source_target_pairs={{0,1},{1,2},{2,3},{4,5},{5,6},{6,7},{8,9},{9,10},{10,11},{12,13},{... | collective-permute-start | bytes 884744 | tf_op jit(solution)/shard_map/ppermute | solution.py:21
  166.1 11.4 %collective-permute-start.12 = (f32[16,1,32,256]{3,0,2,1:T(8,128)S(1)}, f32[16,1,32,256]{3,0,2,1:T(8,128)S(1)}, u32[]{:S(2)}, u32[]{:S(2)}) collective-permute-start(f32[16,1,32,256]{3,0,2,1:T(8,128)S(1)} %get-tuple-element.37), channel_id=1, source_target_pairs={{4,0},{8,4},{12,8},{16,12},{20,16},{24,20},{28,24},{5,1},{9,5},{13... | collective-permute-start | bytes 1572872 | tf_op jit(solution)/shard_map/ppermute | solution.py:23
  167.4 11.6 %collective-permute-start.13 = (f32[16,1,32,256]{3,0,2,1:T(8,128)S(1)}, f32[16,1,32,256]{3,0,2,1:T(8,128)S(1)}, u32[]{:S(2)}, u32[]{:S(2)}) collective-permute-start(f32[16,1,32,256]{3,0,2,1:T(8,128)S(1)} %get-tuple-element.36), channel_id=1, source_target_pairs={{0,4},{4,8},{8,12},{12,16},{16,20},{20,24},{24,28},{1,5},{5,9},{9,... | collective-permute-start | bytes 1572872 | tf_op jit(solution)/shard_map/ppermute | solution.py:21
  181.4 9.1 %collective-permute-start.15 = (f32[16,18,1,256]{3,0,2,1:T(8,128)S(1)}, f32[16,18,1,256]{3,0,2,1:T(8,128)S(1)}, u32[]{:S(2)}, u32[]{:S(2)}) collective-permute-start(f32[16,18,1,256]{3,0,2,1:T(8,128)S(1)} %get-tuple-element.21), channel_id=1, source_target_pairs={{0,1},{1,2},{2,3},{4,5},{5,6},{6,7},{8,9},{9,10},{10,11},{12,13},{... | collective-permute-start | bytes 884744 | tf_op jit(solution)/shard_map/ppermute | solution.py:21
  214.8 11.1 %collective-permute-start.16 = (f32[16,1,32,256]{3,0,2,1:T(8,128)S(1)}, f32[16,1,32,256]{3,0,2,1:T(8,128)S(1)}, u32[]{:S(2)}, u32[]{:S(2)}) collective-permute-start(f32[16,1,32,256]{3,0,2,1:T(8,128)S(1)} %get-tuple-element.35), channel_id=1, source_target_pairs={{4,0},{8,4},{12,8},{16,12},{20,16},{24,20},{28,24},{5,1},{9,5},{13... | collective-permute-start | bytes 1572872 | tf_op jit(solution)/shard_map/ppermute | solution.py:23
  216.1 11.3 %collective-permute-start.17 = (f32[16,1,32,256]{3,0,2,1:T(8,128)S(1)}, f32[16,1,32,256]{3,0,2,1:T(8,128)S(1)}, u32[]{:S(2)}, u32[]{:S(2)}) collective-permute-start(f32[16,1,32,256]{3,0,2,1:T(8,128)S(1)} %get-tuple-element.34), channel_id=1, source_target_pairs={{0,4},{4,8},{8,12},{12,16},{16,20},{20,24},{24,28},{1,5},{5,9},{9,... | collective-permute-start | bytes 1572872 | tf_op jit(solution)/shard_map/ppermute | solution.py:21
  228.7 9.1 %collective-permute-start.19 = (f32[16,18,1,256]{3,0,2,1:T(8,128)S(1)}, f32[16,18,1,256]{3,0,2,1:T(8,128)S(1)}, u32[]{:S(2)}, u32[]{:S(2)}) collective-permute-start(f32[16,18,1,256]{3,0,2,1:T(8,128)S(1)} %get-tuple-element.19), channel_id=1, source_target_pairs={{0,1},{1,2},{2,3},{4,5},{5,6},{6,7},{8,9},{9,10},{10,11},{12,13},{... | collective-permute-start | bytes 884744 | tf_op jit(solution)/shard_map/ppermute | solution.py:21
  252.2 11.1 %collective-permute-start.20 = (f32[16,1,32,256]{3,0,2,1:T(8,128)S(1)}, f32[16,1,32,256]{3,0,2,1:T(8,128)S(1)}, u32[]{:S(2)}, u32[]{:S(2)}) collective-permute-start(f32[16,1,32,256]{3,0,2,1:T(8,128)S(1)} %get-tuple-element.33), channel_id=1, source_target_pairs={{4,0},{8,4},{12,8},{16,12},{20,16},{24,20},{28,24},{5,1},{9,5},{13... | collective-permute-start | bytes 1572872 | tf_op jit(solution)/shard_map/ppermute | solution.py:23
  253.5 11.3 %collective-permute-start.21 = (f32[16,1,32,256]{3,0,2,1:T(8,128)S(1)}, f32[16,1,32,256]{3,0,2,1:T(8,128)S(1)}, u32[]{:S(2)}, u32[]{:S(2)}) collective-permute-start(f32[16,1,32,256]{3,0,2,1:T(8,128)S(1)} %get-tuple-element.32), channel_id=1, source_target_pairs={{0,4},{4,8},{8,12},{12,16},{16,20},{20,24},{24,28},{1,5},{5,9},{9,... | collective-permute-start | bytes 1572872 | tf_op jit(solution)/shard_map/ppermute | solution.py:21
  267.1 9.1 %collective-permute-start.23 = (f32[16,18,1,256]{3,0,2,1:T(8,128)S(1)}, f32[16,18,1,256]{3,0,2,1:T(8,128)S(1)}, u32[]{:S(2)}, u32[]{:S(2)}) collective-permute-start(f32[16,18,1,256]{3,0,2,1:T(8,128)S(1)} %get-tuple-element.17), channel_id=1, source_target_pairs={{0,1},{1,2},{2,3},{4,5},{5,6},{6,7},{8,9},{9,10},{10,11},{12,13},{... | collective-permute-start | bytes 884744 | tf_op jit(solution)/shard_map/ppermute | solution.py:21
  300.2 12.6 %collective-permute-start.24 = (f32[16,1,32,256]{3,0,2,1:T(8,128)S(1)}, f32[16,1,32,256]{3,0,2,1:T(8,128)S(1)}, u32[]{:S(2)}, u32[]{:S(2)}) collective-permute-start(f32[16,1,32,256]{3,0,2,1:T(8,128)S(1)} %get-tuple-element.31), channel_id=1, source_target_pairs={{4,0},{8,4},{12,8},{16,12},{20,16},{24,20},{28,24},{5,1},{9,5},{13... | collective-permute-start | bytes 1572872 | tf_op jit(solution)/shard_map/ppermute | solution.py:23
  301.5 12.8 %collective-permute-start.25 = (f32[16,1,32,256]{3,0,2,1:T(8,128)S(1)}, f32[16,1,32,256]{3,0,2,1:T(8,128)S(1)}, u32[]{:S(2)}, u32[]{:S(2)}) collective-permute-start(f32[16,1,32,256]{3,0,2,1:T(8,128)S(1)} %get-tuple-element.30), channel_id=1, source_target_pairs={{0,4},{4,8},{8,12},{12,16},{16,20},{20,24},{24,28},{1,5},{5,9},{9,... | collective-permute-start | bytes 1572872 | tf_op jit(solution)/shard_map/ppermute | solution.py:21
  316.7 8.9 %collective-permute-start.27 = (f32[16,18,1,256]{3,0,2,1:T(8,128)S(1)}, f32[16,18,1,256]{3,0,2,1:T(8,128)S(1)}, u32[]{:S(2)}, u32[]{:S(2)}) collective-permute-start(f32[16,18,1,256]{3,0,2,1:T(8,128)S(1)} %get-tuple-element.15), channel_id=1, source_target_pairs={{0,1},{1,2},{2,3},{4,5},{5,6},{6,7},{8,9},{9,10},{10,11},{12,13},{... | collective-permute-start | bytes 884744 | tf_op jit(solution)/shard_map/ppermute | solution.py:21
  349.6 15.5 %collective-permute-start.28 = (f32[16,1,32,256]{3,0,2,1:T(8,128)S(1)}, f32[16,1,32,256]{3,0,2,1:T(8,128)S(1)}, u32[]{:S(2)}, u32[]{:S(2)}) collective-permute-start(f32[16,1,32,256]{3,0,2,1:T(8,128)S(1)} %get-tuple-element.29), channel_id=1, source_target_pairs={{4,0},{8,4},{12,8},{16,12},{20,16},{24,20},{28,24},{5,1},{9,5},{13... | collective-permute-start | bytes 1572872 | tf_op jit(solution)/shard_map/ppermute | solution.py:23
  350.9 15.4 %collective-permute-start.29 = (f32[16,1,32,256]{3,0,2,1:T(8,128)S(1)}, f32[16,1,32,256]{3,0,2,1:T(8,128)S(1)}, u32[]{:S(2)}, u32[]{:S(2)}) collective-permute-start(f32[16,1,32,256]{3,0,2,1:T(8,128)S(1)} %get-tuple-element.28), channel_id=1, source_target_pairs={{0,4},{4,8},{8,12},{12,16},{16,20},{20,24},{24,28},{1,5},{5,9},{9,... | collective-permute-start | bytes 1572872 | tf_op jit(solution)/shard_map/ppermute | solution.py:21
  436.0 51.2 %all-to-all-start = ((f32[32,1,128]{2,1,0:T(1,128)}), f32[32,1,128]{2,1,0:T(1,128)S(1)}, u32[]{:S(2)}, u32[]{:S(2)}) async-start(f32[32,1,128]{2,1,0:T(1,128)} %reshape.93), calls=%async_computation | async-start | bytes 32768 | tf_op jit(solution)/shard_map/all_to_all | solution.py:76
  (17 other events, 298.4 us)
where the time goes:
time: 538 us; the launch traced here: 530 us
  other arithmetic  190 us (35%)
  starting transfers between devices  178 us (33%)
  local copies, waits for them, and re-layouts  79 us (15%)
  blocking collectives  40.6 us (8%)
  waiting for transfers between devices  39.7 us (7%)
    select_n x8, other arithmetic, relax(): return jnp.where(diffusion > 0.0, updated, 0.0)  180 us
    ppermute x16, starting transfers between devices, padded_2(): lax.ppermute(tail, axis, [(i, (i + 1) % count) for i in range(ends)])  118 us
    psum x1, blocking collectives, body(): lax.psum(jnp.dot(goal_block.T, goal_block, precision=lax.Precision.HIGHES...  40.6 us
    all_to_all x1, starting transfers between devices, body(): lax.all_to_all(outgoing, ('gx', 'gy'), split_axis=0, concat_axis=0, tiled...  39.6 us
    unnamed x22, local copies, waits for them, and re-layouts  33.4 us
    select_n x1, local copies, waits for them, and re-layouts, relax(): return jnp.where(diffusion > 0.0, updated, 0.0)  32.9 us
    ppermute x16, waiting for transfers between devices, padded_2(): lax.ppermute(tail, axis, [(i, (i + 1) % count) for i in range(ends)])  21.8 us
    ppermute x16, starting transfers between devices, padded_2(): lax.ppermute(head, axis, [((i + 1) % count, i) for i in range(ends)])  20.8 us
  transfers between devices with their start and end apart: 33, of which 22 were waited for; matrix products, arithmetic and copies ran while one was open for 5% of the time, Pallas kernels for 0%

commit v1 on v0

v1 whole, which is shorter than its diff:
```python
import jax
import jax.numpy as jnp
from jax import lax
from jax.experimental import pallas as pl
from jax.experimental.pallas import tpu as pltpu
from jax.sharding import PartitionSpec as P

STEPS = 2
SWEEPS = 4

time_step = 2.0

LANES = 8
CHUNK = 4


def schedule():
    plan, read = [], 0
    for _ in range(STEPS):
        source = read
        others = [b for b in range(3) if b != source]
        for k in range(SWEEPS):
            written = others[k % 2]
            plan.append((read, source, written))
            read = written
    return plan


def sweeps_kernel(wind, field, inverse, mixing, out, held, inv, mix, load_sem, store_sem, send_sem, recv_sem):
    groups, nx, ny = field.shape[0], field.shape[1], field.shape[2]
    nz = field.shape[4]
    gx, gy = lax.axis_index("gx"), lax.axis_index("gy")
    n_gx, n_gy = lax.axis_size("gx"), lax.axis_size("gy")
    xs, ys = pl.ds(1, nx), pl.ds(1, ny)

    loads = [pltpu.make_async_copy(field.at[g], held.at[0, g, xs, ys], load_sem.at[g]) for g in range(groups)]
    loads.append(pltpu.make_async_copy(inverse, inv, load_sem.at[groups]))
    loads.append(pltpu.make_async_copy(mixing, mix, load_sem.at[groups + 1]))
    for copy in loads:
        copy.start()

    row = jnp.zeros((ny + 2, LANES, nz), jnp.float32)
    for b in range(3):
        for g in range(groups):
            held[b, g, 0] = row
            held[b, g, nx + 1] = row
            held[b, g, xs, 0] = row[:nx] if nx <= ny + 2 else jnp.zeros((nx, LANES, nz), jnp.float32)
            held[b, g, xs, ny + 1] = row[:nx] if nx <= ny + 2 else jnp.zeros((nx, LANES, nz), jnp.float32)

    routes = (
        (gx < n_gx - 1, gx > 0, (gx + 1, gy)),
        (gx > 0, gx < n_gx - 1, (gx - 1, gy)),
        (gy < n_gy - 1, gy > 0, (gx, gy + 1)),
        (gy > 0, gy < n_gy - 1, (gx, gy - 1)),
    )
    barrier = pltpu.get_barrier_semaphore()
    for there, _, target in routes:
        @pl.when(there)
        def _():
            pl.semaphore_signal(barrier, inc=1, device_id=target, device_id_type=pl.DeviceIdType.MESH)
    peers = sum(there.astype(jnp.int32) for there, _, _ in routes)
    pl.semaphore_wait(barrier, peers)

    def face(d, b, g, turn):
        if d == 0:
            src, dst = held.at[b, g, nx, ys], held.at[b, g, 0, ys]
        elif d == 1:
            src, dst = held.at[b, g, 1, ys], held.at[b, g, nx + 1, ys]
        elif d == 2:
            src, dst = held.at[b, g, xs, ny], held.at[b, g, xs, 0]
        else:
            src, dst = held.at[b, g, xs, 1], held.at[b, g, xs, ny + 1]
        return pltpu.make_async_remote_copy(
            src_ref=src,
            dst_ref=dst,
            send_sem=send_sem.at[turn % 2, g, d],
            recv_sem=recv_sem.at[turn % 2, g, d],
            device_id=routes[d][2],
            device_id_type=pl.DeviceIdType.MESH,
        )

    def start(d, b, g, turn):
        @pl.when(routes[d][0])
        def _():
            face(d, b, g, turn).start()

    def wait_send(d, b, g, turn):
        @pl.when(routes[d][0])
        def _():
            face(d, b, g, turn).wait_send()

    def wait_recv(d, b, g, turn):
        @pl.when(routes[d][1])
        def _():
            face(d, b, g, turn).wait_recv()

    w0, w1, w2 = wind[0], wind[1], wind[2]
    lane = lax.broadcasted_iota(jnp.int32, (CHUNK, LANES, nz), 2)

    def plane(x, g, read, source, written):
        def chunk(k, carry):
            y = 1 + k * CHUNK
            centre = held[read, g, x, pl.ds(y, CHUNK)]
            x_low = held[read, g, x - 1, pl.ds(y, CHUNK)]
            x_high = held[read, g, x + 1, pl.ds(y, CHUNK)]
            y_low = held[read, g, x, pl.ds(y - 1, CHUNK)]
            y_high = held[read, g, x, pl.ds(y + 1, CHUNK)]
            z_low = jnp.where(lane == 0, 0.0, pltpu.roll(centre, 1, 2))
            z_high = jnp.where(lane == nz - 1, 0.0, pltpu.roll(centre, nz - 1, 2))
            beside = (x_low + x_high) + (y_low + y_high) + (z_low + z_high)
            upwind = w0 * x_low + w1 * y_low + w2 * z_low
            start_value = held[source, g, x, pl.ds(y, CHUNK)]
            r = inv[x - 1, pl.ds(y - 1, CHUNK)]
            a = mix[x - 1, pl.ds(y - 1, CHUNK)]
            held[written, g, x, pl.ds(y, CHUNK)] = (start_value + upwind) * r + a * beside
            return carry

        lax.fori_loop(0, ny // CHUNK, chunk, 0)

    plan = schedule()
    last = len(plan)
    for g in range(groups):
        loads[g].wait()
        for d in range(4):
            start(d, 0, g, 0)
    loads[groups].wait()
    loads[groups + 1].wait()

    stores = []
    for turn, (read, source, written) in enumerate(plan, 1):
        for g in range(groups):
            for d in range(4):
                wait_recv(d, read, g, turn - 1)
                if turn >= 2:
                    wait_send(d, plan[turn - 3][2] if turn >= 3 else 0, g, turn - 2)
            ends = (1, nx) if nx > 1 else (1,)
            for x in ends:
                plane(x, g, read, source, written)
            if turn < last:
                for d in (0, 1):
                    start(d, written, g, turn)

            def inner(x, carry):
                plane(x, g, read, source, written)
                return carry

            lax.fori_loop(2, nx, inner, 0)
            if turn < last:
                for d in (2, 3):
                    start(d, written, g, turn)
            else:
                stores.append(pltpu.make_async_copy(held.at[written, g, xs, ys], out.at[g], store_sem.at[g]))
                stores[-1].start()
    for g in range(groups):
        for d in range(4):
            wait_send(d, plan[last - 1][0], g, last - 1)
        stores[g].wait()


def run_sweeps(wind, field, inverse, mixing):
    groups, nx, ny, _, nz = field.shape
    hbm = pl.BlockSpec(memory_space=pl.ANY)
    return pl.pallas_call(
        sweeps_kernel,
        out_shape=jax.ShapeDtypeStruct(field.shape, jnp.float32),
        in_specs=[pl.BlockSpec(memory_space=pltpu.SMEM), hbm, hbm, hbm],
        out_specs=hbm,
        scratch_shapes=[
            pltpu.VMEM((3, groups, nx + 2, ny + 2, LANES, nz), jnp.float32),
            pltpu.VMEM((nx, ny, LANES, nz), jnp.float32),
            pltpu.VMEM((nx, ny, LANES, nz), jnp.float32),
            pltpu.SemaphoreType.DMA((groups + 2,)),
            pltpu.SemaphoreType.DMA((groups,)),
            pltpu.SemaphoreType.DMA((2, groups, 4)),
            pltpu.SemaphoreType.DMA((2, groups, 4)),
        ],
        compiler_params=pltpu.CompilerParams(
            collective_id=0, has_side_effects=True, vmem_limit_bytes=60 * 1024 * 1024
        ),
    )(wind, field, inverse, mixing)


def body(probes, diffusivity, wind_speed, sensor_cell, sensor_owner, sensor_count, goal_weight):
    probe_count, nx, ny, nz = probes.shape
    groups = probe_count // LANES
    field = probes.reshape(groups, LANES, nx, ny, nz).transpose(0, 2, 3, 1, 4)
    inverse = 1.0 / (
        1.0 + time_step * (6.0 * diffusivity + wind_speed[0] + wind_speed[1] + wind_speed[2])
    )
    mixing = time_step * diffusivity * inverse
    wide = (nx, ny, LANES, nz)
    state = run_sweeps(
        time_step * wind_speed,
        field,
        jnp.broadcast_to(inverse[:, :, None, :], wide),
        jnp.broadcast_to(mixing[:, :, None, :], wide),
    )
    fields = state.transpose(0, 3, 1, 2, 4).reshape(probes.shape)

    sensor_rows = sensor_cell.shape[2]
    goal_count = goal_weight.shape[3]
    device_count = lax.axis_size("gx") * lax.axis_size("gy")
    cells = sensor_cell.reshape(-1)
    columns = jnp.take(state.reshape(groups, nx * ny, LANES, nz), cells // nz, axis=1, mode="clip")
    here = jnp.arange(nz, dtype=jnp.int32)[None, :] == (cells % nz)[:, None]
    readings = jnp.sum(jnp.where(here[None, :, None, :], columns, 0.0), axis=3)
    readings = readings.transpose(1, 0, 2).reshape(sensor_rows, probe_count)
    active = jnp.arange(sensor_rows, dtype=jnp.int32) < sensor_count.reshape(())
    readings = jnp.where(active[:, None], readings, 0.0)
    payload = jnp.concatenate(
        [
            readings,
            goal_weight.reshape(sensor_rows, goal_count),
            sensor_owner.reshape(sensor_rows, 1).astype(jnp.float32),
        ],
        axis=1,
    )
    everyone = lax.all_gather(payload, ("gx", "gy"), axis=0, tiled=True)
    all_readings = everyone[:, :probe_count]
    all_weights = everyone[:, probe_count : probe_count + goal_count]
    owners = everyone[:, probe_count + goal_count].astype(jnp.int32)
    onehot = (owners[:, None] == jnp.arange(device_count, dtype=jnp.int32)[None, :]).astype(jnp.float32)
    outer = (all_weights[:, :, None] * all_readings[:, None, :]).reshape(-1, goal_count * probe_count)
    goals = jnp.dot(onehot.T, outer, precision=lax.Precision.HIGHEST)
    goals = goals.reshape(device_count * goal_count, probe_count)
    ritz_gram = jnp.dot(goals.T, goals, precision=lax.Precision.HIGHEST)
    mine = lax.axis_index("gx") * lax.axis_size("gy") + lax.axis_index("gy")
    goal_block = lax.dynamic_slice_in_dim(goals, mine * goal_count, goal_count, axis=0)
    return (fields, goal_block, ritz_gram)


def solution(mesh):
    placed = (
        P(None, "gx", "gy", None),
        P("gx", "gy", None),
        P(),
        P("gx", "gy", None),
        P("gx", "gy", None, None),
        P("gx", "gy"),
        P("gx", "gy", None, None),
    )
    return jax.shard_map(
        body,
        mesh=mesh,
        in_specs=placed,
        out_specs=(P(None, "gx", "gy", None), P(("gx", "gy"), None), P()),
        check_vma=False,
    )
```

time: 538 us -> 315 us (0.59); the launches traced: 530 us -> 313 us
  Pallas kernels: 0 us -> 198 us
  other arithmetic: 190 us -> 4.75 us
  starting transfers between devices: 178 us -> 0 us
  local copies, waits for them, and re-layouts: 79 us -> 32.9 us
  waiting for transfers between devices: 39.7 us -> 0 us
  blocking collectives: 40.6 us -> 71.7 us
    pallas_call x0 -> x1, Pallas kernels: none -> 198 us  [run_sweeps(): pl.pallas_call(sweeps_kernel, out_shape=jax.ShapeDtypeStruct(field.shape,...]
    select_n x9 -> x3, other arithmetic: 180 us -> 0.02 us  [the longest x1 0.01 us: body(): cells // nz]
    ppermute x32 -> x0, starting transfers between devices: 138 us -> none  [the longest x16 118 us: padded_2(): lax.ppermute(tail, axis, [(i, (i + 1) % count) for i in range(ends)])]
    all_gather x0 -> x1, blocking collectives: none -> 71.7 us  [body(): everyone = lax.all_gather(payload, ('gx', 'gy'), axis=0, tiled=True)]
    psum x1 -> x0, blocking collectives: 40.6 us -> none  [body(): lax.psum(jnp.dot(goal_block.T, goal_block, precision=lax.Precision.HIGHES...]
    ppermute x32 -> x0, waiting for transfers between devices: 39.7 us -> none  [the longest x16 21.8 us: padded_2(): lax.ppermute(tail, axis, [(i, (i + 1) % count) for i in range(ends)])]
    all_to_all x1 -> x0, starting transfers between devices: 39.6 us -> none  [body(): lax.all_to_all(outgoing, ('gx', 'gy'), split_axis=0, concat_axis=0, tiled...]
    select_n x1 -> x0, local copies, waits for them, and re-layouts: 32.9 us -> none  [relax(): return jnp.where(diffusion > 0.0, updated, 0.0)]
  transfers between devices with their start and end apart: 33 -> 0, of which waited for: 22 -> 0; matrix products, arithmetic and copies ran while one was open for 5% -> 0% of each run, Pallas kernels for 0% -> 0%
where the time goes in v1:
time: 315 us; the launch traced here: 313 us
  Pallas kernels  198 us (63%)
  blocking collectives  71.7 us (23%)
  local copies, waits for them, and re-layouts  32.9 us (10%)
  other arithmetic  4.75 us (2%)
  matrix products  3.36 us (1%)
    pallas_call x1, Pallas kernels, run_sweeps(): pl.pallas_call(sweeps_kernel, out_shape=jax.ShapeDtypeStruct(field.shape,...  198 us
    all_gather x1, blocking collectives, body(): everyone = lax.all_gather(payload, ('gx', 'gy'), axis=0, tiled=True)  71.7 us
    reshape x1, local copies, waits for them, and re-layouts, body(): field = probes.reshape(groups, LANES, nx, ny, nz).transpose(0, 2, 3, 1, 4)  11 us
    transpose x1, local copies, waits for them, and re-layouts, body(): fields = state.transpose(0, 3, 1, 2, 4).reshape(probes.shape)  9.26 us

profile of v1, /device:TPU:0, one launch (start us, length us, event | category | flops | bytes accessed | tf_op | source)
XLA Modules:
  0.0 312.6 jit_solution(954531534585958296)
XLA Ops:
  0.6 1.4 fusion.5
  2.0 3.1 %multiply_multiply_fusion = (f32[16,32,256]{2,1,0:T(8,128)S(1)}, f32[16,32,256]{2,1,0:T(8,128)S(1)}) fusion(f32[16,32,256]{2,1,0:T(8,128)} %param.8, f32[]{:T(128)} %bitcast.4, f32[]{:T(128)} %bitcast.3, f32[]{:T(128)} %bitcast.2), kind=kLoop, calls=%fused_computation.5 | loop fusion | flops 1179648 | bytes 1572876 | tf_op jit(solution)/shard_map/mul | solution.py:190
  5.1 0.0 copy-start
  5.1 2.4 broadcast_in_dim.30.inverse
  7.6 2.4 broadcast_in_dim.31.mixing
  10.0 1.5 copy-done
  11.6 11.0 %copy.24 = f32[2,8,16,32,256]{4,1,3,2,0:T(8,128)} copy(f32[2,8,16,32,256]{4,3,2,1,0:T(8,128)S(1)} %bitcast.40) | data formatting | bytes 16777216 | tf_op jit(solution)/shard_map/reshape | solution.py:186
  22.5 0.0 copy-done.2
  22.5 0.5 broadcast_multiply_fusion.1.wind
  23.0 198.5 %shard_map.94 = f32[2,16,32,8,256]{4,3,2,1,0:T(8,128)} custom-call(f32[3]{0:T(128)} %broadcast_multiply_fusion.1.wind, f32[2,16,32,8,256]{4,3,2,1,0:T(8,128)} %bitcast.38, f32[16,32,8,256]{3,2,1,0:T(8,128)} %broadcast_in_dim.30.inverse, f32[16,32,8,256]{3,2,1,0:T(8,128)} %broadcast_in_dim.31.mixing), custom_call_target="tpu_custom_call" | custom-call | tf_op jit(solution)/shard_map/pallas_call | solution.py:163
  221.5 0.0 copy-start.4
  221.5 0.0 copy-start.1
  221.6 4.1 %gather_fusion = f32[128,2,8,256]{3,2,1,0:T(8,128)S(1)} fusion(f32[2,512,8,256]{3,2,1,0:T(8,128)} %bitcast.36, s32[1024]{0:T(1024)S(1)} %pad_clamp_fusion), kind=kCustom, calls=%fused_computation | custom fusion | bytes 4194816 | tf_op jit(solution)/shard_map/jit(_take)/gather | solution.py:204
  225.7 0.1 iota_compare_fusion.2
  225.7 0.5 select_reduce_fusion
  226.2 0.1 copy.22
  227.0 0.0 copy-done.4
  227.0 71.7 %all_gather.3 = f32[4096,33]{0,1:T(8,128)S(1)} all-gather(f32[128,33]{0,1:T(8,128)S(1)} %pad_maximum_fusion), channel_id=1, replica_groups=mesh['gx'=8,'gy'=4] {'gx','gy'}, dimensions={0}, use_global_device_ids=true | all-gather | bytes 557568 | tf_op jit(solution)/shard_map/all_gather | solution.py:218
  298.7 0.5 broadcast_multiply_fusion
  299.2 2.2 fusion
  301.4 0.1 reshape.175
  301.6 0.6 constant_dynamic-slice_fusion
  302.2 1.2 fusion.6
  303.3 9.3 %copy.21 = f32[2,8,16,32,256]{4,3,2,1,0:T(8,128)} copy(f32[2,8,16,32,256]{4,1,3,2,0:T(8,128)} %bitcast.37) | data formatting | bytes 16777216 | tf_op jit(solution)/shard_map/transpose | solution.py:198
  (13 shorter events, 0.1 us)
Async XLA Ops:
  5.1 6.4 %copy-start = (f32[16,16,32,256]{3,2,1,0:T(8,128)S(1)}, f32[16,16,32,256]{3,2,1,0:T(8,128)}, u32[]{:S(2)}) copy-start(f32[16,16,32,256]{3,2,1,0:T(8,128)} %param.7) | copy-start | bytes 25165828
  11.5 11.0 %copy-start.2 = (f32[3]{0:T(128)S(1)}, f32[3]{0:T(128)}, u32[]{:S(2)}) copy-start(f32[3]{0:T(128)} %param.9) | copy-start | bytes 40
  23.0 198.5 %copy-start.3 = (s32[1,1,128]{2,1,0:T(1,128)S(1)}, s32[1,1,128]{2,1,0:T(1,128)}, u32[]{:S(2)}) copy-start(s32[1,1,128]{2,1,0:T(1,128)} %param.10) | copy-start | bytes 1540
  221.5 5.5 %copy-start.4 = (s32[1,1,128,1]{2,3,1,0:T(1,128)S(1)}, s32[1,1,128,1]{2,3,1,0:T(1,128)}, u32[]{:S(2)}) copy-start(s32[1,1,128,1]{2,3,1,0:T(1,128)} %param.11) | copy-start | bytes 1540
  221.5 5.5 %copy-start.1 = (f32[1,1,128,16]{2,3,1,0:T(8,128)S(1)}, f32[1,1,128,16]{2,3,1,0:T(8,128)}, u32[]{:S(2)}) copy-start(f32[1,1,128,16]{2,3,1,0:T(8,128)} %param.13) | copy-start | bytes 24580

commit v2 on v1

--- a/solution.py
+++ b/solution.py
@@ -26,14 +26,15 @@
     return plan
 
 
-def sweeps_kernel(wind, field, inverse, mixing, out, held, inv, mix, load_sem, store_sem, send_sem, recv_sem):
+def sweeps_kernel(wind, field, inverse, mixing, out, held0, held1, held2, inv, mix, load_sem, store_sem, send_sem, recv_sem):
+    held = (held0, held1, held2)
     groups, nx, ny = field.shape[0], field.shape[1], field.shape[2]
     nz = field.shape[4]
     gx, gy = lax.axis_index("gx"), lax.axis_index("gy")
     n_gx, n_gy = lax.axis_size("gx"), lax.axis_size("gy")
     xs, ys = pl.ds(1, nx), pl.ds(1, ny)
 
-    loads = [pltpu.make_async_copy(field.at[g], held.at[0, g, xs, ys], load_sem.at[g]) for g in range(groups)]
+    loads = [pltpu.make_async_copy(field.at[g], held[0].at[g, xs, ys], load_sem.at[g]) for g in range(groups)]
     loads.append(pltpu.make_async_copy(inverse, inv, load_sem.at[groups]))
     loads.append(pltpu.make_async_copy(mixing, mix, load_sem.at[groups + 1]))
     for copy in loads:
@@ -42,10 +43,10 @@
     row = jnp.zeros((ny + 2, LANES, nz), jnp.float32)
     for b in range(3):
         for g in range(groups):
-            held[b, g, 0] = row
-            held[b, g, nx + 1] = row
-            held[b, g, xs, 0] = row[:nx] if nx <= ny + 2 else jnp.zeros((nx, LANES, nz), jnp.float32)
-            held[b, g, xs, ny + 1] = row[:nx] if nx <= ny + 2 else jnp.zeros((nx, LANES, nz), jnp.float32)
+            held[b][g, 0] = row
+            held[b][g, nx + 1] = row
+            held[b][g, xs, 0] = row[:nx] if nx <= ny + 2 else jnp.zeros((nx, LANES, nz), jnp.float32)
+            held[b][g, xs, ny + 1] = row[:nx] if nx <= ny + 2 else jnp.zeros((nx, LANES, nz), jnp.float32)
 
     routes = (
         (gx < n_gx - 1, gx > 0, (gx + 1, gy)),
@@ -63,13 +64,13 @@
 
     def face(d, b, g, turn):
         if d == 0:
-            src, dst = held.at[b, g, nx, ys], held.at[b, g, 0, ys]
+            src, dst = held[b].at[g, nx, ys], held[b].at[g, 0, ys]
         elif d == 1:
-            src, dst = held.at[b, g, 1, ys], held.at[b, g, nx + 1, ys]
+            src, dst = held[b].at[g, 1, ys], held[b].at[g, nx + 1, ys]
         elif d == 2:
-            src, dst = held.at[b, g, xs, ny], held.at[b, g, xs, 0]
+            src, dst = held[b].at[g, xs, ny], held[b].at[g, xs, 0]
         else:
-            src, dst = held.at[b, g, xs, 1], held.at[b, g, xs, ny + 1]
+            src, dst = held[b].at[g, xs, 1], held[b].at[g, xs, ny + 1]
         return pltpu.make_async_remote_copy(
             src_ref=src,
             dst_ref=dst,
@@ -98,24 +99,20 @@
     lane = lax.broadcasted_iota(jnp.int32, (CHUNK, LANES, nz), 2)
 
     def plane(x, g, read, source, written):
-        def chunk(k, carry):
-            y = 1 + k * CHUNK
-            centre = held[read, g, x, pl.ds(y, CHUNK)]
-            x_low = held[read, g, x - 1, pl.ds(y, CHUNK)]
-            x_high = held[read, g, x + 1, pl.ds(y, CHUNK)]
-            y_low = held[read, g, x, pl.ds(y - 1, CHUNK)]
-            y_high = held[read, g, x, pl.ds(y + 1, CHUNK)]
+        for y in range(1, ny + 1, CHUNK):
+            centre = held[read][g, x, pl.ds(y, CHUNK)]
+            x_low = held[read][g, x - 1, pl.ds(y, CHUNK)]
+            x_high = held[read][g, x + 1, pl.ds(y, CHUNK)]
+            y_low = held[read][g, x, pl.ds(y - 1, CHUNK)]
+            y_high = held[read][g, x, pl.ds(y + 1, CHUNK)]
             z_low = jnp.where(lane == 0, 0.0, pltpu.roll(centre, 1, 2))
             z_high = jnp.where(lane == nz - 1, 0.0, pltpu.roll(centre, nz - 1, 2))
             beside = (x_low + x_high) + (y_low + y_high) + (z_low + z_high)
             upwind = w0 * x_low + w1 * y_low + w2 * z_low
-            start_value = held[source, g, x, pl.ds(y, CHUNK)]
+            start_value = held[source][g, x, pl.ds(y, CHUNK)]
             r = inv[x - 1, pl.ds(y - 1, CHUNK)]
             a = mix[x - 1, pl.ds(y - 1, CHUNK)]
-            held[written, g, x, pl.ds(y, CHUNK)] = (start_value + upwind) * r + a * beside
-            return carry
-
-        lax.fori_loop(0, ny // CHUNK, chunk, 0)
+            held[written][g, x, pl.ds(y, CHUNK)] = (start_value + upwind) * r + a * beside
 
     plan = schedule()
     last = len(plan)
@@ -133,9 +130,11 @@
                 wait_recv(d, read, g, turn - 1)
                 if turn >= 2:
                     wait_send(d, plan[turn - 3][2] if turn >= 3 else 0, g, turn - 2)
-            ends = (1, nx) if nx > 1 else (1,)
-            for x in ends:
-                plane(x, g, read, source, written)
+            def end(i, carry):
+                plane(1 + i * (nx - 1), g, read, source, written)
+                return carry
+
+            lax.fori_loop(0, 2, end, 0)
             if turn < last:
                 for d in (0, 1):
                     start(d, written, g, turn)
@@ -149,7 +148,7 @@
                 for d in (2, 3):
                     start(d, written, g, turn)
             else:
-                stores.append(pltpu.make_async_copy(held.at[written, g, xs, ys], out.at[g], store_sem.at[g]))
+                stores.append(pltpu.make_async_copy(held[written].at[g, xs, ys], out.at[g], store_sem.at[g]))
                 stores[-1].start()
     for g in range(groups):
         for d in range(4):
@@ -166,7 +165,7 @@
         in_specs=[pl.BlockSpec(memory_space=pltpu.SMEM), hbm, hbm, hbm],
         out_specs=hbm,
         scratch_shapes=[
-            pltpu.VMEM((3, groups, nx + 2, ny + 2, LANES, nz), jnp.float32),
+            *[pltpu.VMEM((groups, nx + 2, ny + 2, LANES, nz), jnp.float32)] * 3,
             pltpu.VMEM((nx, ny, LANES, nz), jnp.float32),
             pltpu.VMEM((nx, ny, LANES, nz), jnp.float32),
             pltpu.SemaphoreType.DMA((groups + 2,)),
@@ -178,6 +177,62 @@
             collective_id=0, has_side_effects=True, vmem_limit_bytes=60 * 1024 * 1024
         ),
     )(wind, field, inverse, mixing)
+
+
+def gather_kernel(payload, out, send_sem, recv_sem):
+    n_gy = lax.axis_size("gy")
+    devices = lax.axis_size("gx") * n_gy
+    me = lax.axis_index("gx") * n_gy + lax.axis_index("gy")
+
+    def place(k):
+        other = (me + k) % devices
+        return (other // n_gy, other % n_gy)
+
+    def greet(k, carry):
+        pl.semaphore_signal(
+            pltpu.get_barrier_semaphore(), inc=1, device_id=place(k), device_id_type=pl.DeviceIdType.MESH
+        )
+        return carry
+
+    lax.fori_loop(1, devices, greet, 0)
+    pl.semaphore_wait(pltpu.get_barrier_semaphore(), devices - 1)
+
+    def copy(k, slot):
+        return pltpu.make_async_remote_copy(
+            src_ref=payload,
+            dst_ref=out.at[slot],
+            send_sem=send_sem.at[k],
+            recv_sem=recv_sem.at[k],
+            device_id=place(k),
+            device_id_type=pl.DeviceIdType.MESH,
+        )
+
+    def send(k, carry):
+        copy(k, me).start()
+        return carry
+
+    def finish(k, carry):
+        arriving = copy(k, (me + devices - k) % devices)
+        arriving.wait_send()
+        arriving.wait_recv()
+        return carry
+
+    lax.fori_loop(1, devices, send, 0)
+    out[me] = payload[...]
+    lax.fori_loop(1, devices, finish, 0)
+
+
+def gather_all(payload):
+    devices = lax.axis_size("gx") * lax.axis_size("gy")
+    vmem = pl.BlockSpec(memory_space=pltpu.VMEM)
+    return pl.pallas_call(
+        gather_kernel,
+        out_shape=jax.ShapeDtypeStruct((devices,) + payload.shape, jnp.float32),
+        in_specs=[vmem],
+        out_specs=vmem,
+        scratch_shapes=[pltpu.SemaphoreType.DMA((devices,)), pltpu.SemaphoreType.DMA((devices,))],
+        compiler_params=pltpu.CompilerParams(collective_id=1, has_side_effects=True),
+    )(payload)
 
 
 def body(probes, diffusivity, wind_speed, sensor_cell, sensor_owner, sensor_count, goal_weight):
@@ -215,7 +270,9 @@
         ],
         axis=1,
     )
-    everyone = lax.all_gather(payload, ("gx", "gy"), axis=0, tiled=True)
+    width = payload.shape[1]
+    payload = jnp.pad(payload.T, ((0, -width % 8), (0, 0)))
+    everyone = gather_all(payload).transpose(0, 2, 1).reshape(device_count * sensor_rows, -1)
     all_readings = everyone[:, :probe_count]
     all_weights = everyone[:, probe_count : probe_count + goal_count]
     owners = everyone[:, probe_count + goal_count].astype(jnp.int32)

time: 315 us -> 168 us (0.53)
  Pallas kernels: 198 us -> 124 us
  blocking collectives: 71.7 us -> 0 us
    pallas_call x1, Pallas kernels: 198 us -> 93.1 us  [run_sweeps(): pl.pallas_call(sweeps_kernel, out_shape=jax.ShapeDtypeStruct(field.shape,...]
    all_gather x1 -> x0, blocking collectives: 71.7 us -> none  [body(): everyone = lax.all_gather(payload, ('gx', 'gy'), axis=0, tiled=True)]
    pallas_call x0 -> x1, Pallas kernels: none -> 30.6 us  [gather_all(): pl.pallas_call(gather_kernel, out_shape=jax.ShapeDtypeStruct((devices,) +...]
where the time goes in v2:
time: 168 us
  Pallas kernels  124 us (74%)
  local copies, waits for them, and re-layouts  34.6 us (21%)
  other arithmetic  4.75 us (3%)
  matrix products  3.36 us (2%)
    pallas_call x1, Pallas kernels, run_sweeps(): pl.pallas_call(sweeps_kernel, out_shape=jax.ShapeDtypeStruct(field.shape,...  93.1 us
    pallas_call x1, Pallas kernels, gather_all(): pl.pallas_call(gather_kernel, out_shape=jax.ShapeDtypeStruct((devices,) +...  30.6 us
    reshape x1, local copies, waits for them, and re-layouts, body(): field = probes.reshape(groups, LANES, nx, ny, nz).transpose(0, 2, 3, 1, 4)  11 us
    transpose x1, local copies, waits for them, and re-layouts, body(): fields = state.transpose(0, 3, 1, 2, 4).reshape(probes.shape)  9.26 us
    gather x1, local copies, waits for them, and re-layouts, body(): jnp.take(state.reshape(groups, nx * ny, LANES, nz), cells // nz, axis=1,...  4.06 us

profile of v2, /device:TPU:0, one launch (start us, length us, event | category | flops | bytes accessed | tf_op | source)
XLA Modules:
  0.0 168.0 jit_solution(12108280021946354981)
XLA Ops:
  0.6 1.4 fusion.5
  2.0 3.1 %multiply_multiply_fusion = (f32[16,32,256]{2,1,0:T(8,128)S(1)}, f32[16,32,256]{2,1,0:T(8,128)S(1)}) fusion(f32[16,32,256]{2,1,0:T(8,128)} %param.8, f32[]{:T(128)} %bitcast.4, f32[]{:T(128)} %bitcast.3, f32[]{:T(128)} %bitcast.2), kind=kLoop, calls=%fused_computation.6 | loop fusion | flops 1179648 | bytes 1572876 | tf_op jit(solution)/shard_map/mul | solution.py:245
  5.1 0.0 copy-start
  5.1 2.4 %broadcast_in_dim.30.inverse = f32[16,32,8,256]{3,2,1,0:T(8,128)} broadcast(f32[16,32,256]{2,1,0:T(8,128)S(1)} %get-tuple-element.6), dimensions={0,1,3} | broadcast | bytes 4718592 | tf_op jit(solution)/shard_map/broadcast_in_dim | solution.py:250
  7.6 2.4 %broadcast_in_dim.31.mixing = f32[16,32,8,256]{3,2,1,0:T(8,128)} broadcast(f32[16,32,256]{2,1,0:T(8,128)S(1)} %get-tuple-element.5), dimensions={0,1,3} | broadcast | bytes 4718592 | tf_op jit(solution)/shard_map/broadcast_in_dim | solution.py:251
  10.0 1.5 copy-done
  11.6 11.0 %copy.24 = f32[2,8,16,32,256]{4,1,3,2,0:T(8,128)} copy(f32[2,8,16,32,256]{4,3,2,1,0:T(8,128)S(1)} %bitcast.48) | data formatting | bytes 16777216 | tf_op jit(solution)/shard_map/reshape | solution.py:241
  22.5 0.5 broadcast_multiply_fusion.1.wind
  23.0 93.1 %shard_map.94 = f32[2,16,32,8,256]{4,3,2,1,0:T(8,128)} custom-call(f32[3]{0:T(128)} %broadcast_multiply_fusion.1.wind, f32[2,16,32,8,256]{4,3,2,1,0:T(8,128)} %bitcast.46, f32[16,32,8,256]{3,2,1,0:T(8,128)} %broadcast_in_dim.30.inverse, f32[16,32,8,256]{3,2,1,0:T(8,128)} %broadcast_in_dim.31.mixing), custom_call_target="tpu_custom_call" | custom-call | tf_op jit(solution)/shard_map/pallas_call | solution.py:162
  116.2 0.0 copy-start.4
  116.2 0.0 copy-start.1
  116.2 4.1 %gather_fusion = f32[128,2,8,256]{3,2,1,0:T(8,128)S(1)} fusion(f32[2,512,8,256]{3,2,1,0:T(8,128)} %bitcast.44, s32[1024]{0:T(1024)S(1)} %pad_clamp_fusion), kind=kCustom, calls=%fused_computation | custom fusion | bytes 4194816 | tf_op jit(solution)/shard_map/jit(_take)/gather | solution.py:259
  120.3 0.1 iota_compare_fusion.2
  120.4 0.5 select_reduce_fusion
  120.9 0.1 copy.19
  121.7 0.6 pad.4.payload
  122.3 30.6 %shard_map.95 = f32[32,40,128]{2,1,0:T(8,128)} custom-call(f32[40,128]{1,0:T(8,128)} %pad.4.payload), custom_call_target="tpu_custom_call" | custom-call | tf_op jit(solution)/shard_map/pallas_call | solution.py:228
  152.9 1.1 copy_bitcast_fusion.1
  154.1 0.5 broadcast_multiply_fusion
  154.6 2.2 %fusion = f32[32,256]{1,0:T(8,128)S(1)} fusion(f32[4096,256]{0,1:T(8,128)S(1)} %bitcast.47, s32[4096]{0:T(1024)S(1)} %bitcast.50), kind=kOutput, calls=%fused_computation.8 | convolution fusion | flops 402784256 | bytes 4243456 | tf_op jit(solution)/shard_map/dot_general | solution.py:281
  156.8 0.1 reshape.179
  156.9 0.6 constant_dynamic-slice_fusion
  157.6 1.2 fusion.6
  158.7 9.3 %copy.18 = f32[2,8,16,32,256]{4,3,2,1,0:T(8,128)} copy(f32[2,8,16,32,256]{4,1,3,2,0:T(8,128)} %bitcast.45) | data formatting | bytes 16777216 | tf_op jit(solution)/shard_map/transpose | solution.py:253
  (15 shorter events, 0.1 us)
Async XLA Ops:
  5.1 6.4 %copy-start = (f32[16,16,32,256]{3,2,1,0:T(8,128)S(1)}, f32[16,16,32,256]{3,2,1,0:T(8,128)}, u32[]{:S(2)}) copy-start(f32[16,16,32,256]{3,2,1,0:T(8,128)} %param.7) | copy-start | bytes 25165828
  11.5 11.0 %copy-start.2 = (f32[3]{0:T(128)S(1)}, f32[3]{0:T(128)}, u32[]{:S(2)}) copy-start(f32[3]{0:T(128)} %param.9) | copy-start | bytes 40
  23.0 93.2 %copy-start.3 = (s32[1,1,128]{2,1,0:T(1,128)S(1)}, s32[1,1,128]{2,1,0:T(1,128)}, u32[]{:S(2)}) copy-start(s32[1,1,128]{2,1,0:T(1,128)} %param.10) | copy-start | bytes 1540
  116.2 5.5 %copy-start.4 = (s32[1,1,128,1]{2,3,1,0:T(1,128)S(1)}, s32[1,1,128,1]{2,3,1,0:T(1,128)}, u32[]{:S(2)}) copy-start(s32[1,1,128,1]{2,3,1,0:T(1,128)} %param.11) | copy-start | bytes 1540
  116.2 5.5 %copy-start.1 = (f32[1,1,128,16]{2,3,1,0:T(8,128)S(1)}, f32[1,1,128,16]{2,3,1,0:T(8,128)}, u32[]{:S(2)}) copy-start(f32[1,1,128,16]{2,3,1,0:T(8,128)} %param.13) | copy-start | bytes 24580
